TPU v7x, 32 devices: a whole 2x2x4 slice. The times are simulated.
32 devices in a mesh: seq: 8 (over z, core), head: 4 (over y, x).
Axes of the slice: x: 2, y: 2, z: 4, core: 2. Of those that a mesh axis runs over, the one named last changes fastest.
Arguments:
- tokens: bfloat16 [1024, 4096], P('seq', 'head'), may hold values from -6 to 6
- w_query: bfloat16 [4096, 4096], P(None, 'head'), may hold values from -0.09375 to 0.09375
- w_key: bfloat16 [4096, 4096], P(None, 'head'), may hold values from -0.09375 to 0.09375
- w_value: bfloat16 [4096, 4096], P(None, 'head'), may hold values from -0.09375 to 0.09375
- upstream: bfloat16 [1024, 4096], P('seq', 'head'), may hold values from -6 to 6
- log_decay: float32 [1024, 32], P('seq', 'head'), may hold values from -1 to 0, as said below
- segment: int32 [1024], replicated, may hold values from 0 to 7, never falling along the last dimension, each value on 1 to 256 neighbouring positions
Outputs:
- grad_query: bfloat16 [4096, 4096], P('seq', 'head')
- grad_key: bfloat16 [4096, 4096], P('seq', 'head')
- grad_value: bfloat16 [4096, 4096], P('seq', 'head')
Inputs may be any that keep to these rules, and one draw needn't show every extreme that they name: log_decay is negative. `segment`: document ids never fall along the tokens; each document holds 1 to 256 tokens.
All inputs are finite; a program needn't handle non-finite values.
Results may differ from a plain program's by a relative error of at most 0.02.
Values may be sent and summed in bfloat16 or wider, within the bound.
No kernel may reach another device: no remote copies, remote signals or barrier semaphores. Data moves between devices by JAX's collectives and lax.ppermute only.
A program may use at most 64 MiB of HBM per device.

v0:
```python
import jax
import jax.numpy as jnp
from jax import lax
from jax.sharding import PartitionSpec as P

HEAD = 128


def carried_in(x, axis, combine, identity, reverse):
    count, place = (lax.axis_size(axis), lax.axis_index(axis))
    everything = jax.tree.map(
        lambda part, kind: lax.all_gather(part.astype(kind), axis), x, (jnp.bfloat16, jnp.bfloat16)
    )
    start = jax.tree.map(
        lambda part, zero: jnp.broadcast_to(jnp.asarray(zero, part.dtype), part.shape), x, identity
    )

    def turn(k, before):
        at = count - 1 - k if reverse else k
        reached = at > place if reverse else at < place
        new = combine(
            before, jax.tree.map(lambda part, own: part[at].astype(own.dtype), everything, x)
        )
        return jax.tree.map(lambda a, b: jnp.where(reached, a, b), new, before)

    return lax.fori_loop(0, count, turn, start)


def block_factors(log_rates, segs, previous):
    log_sum = jnp.cumsum(log_rates, axis=0)
    last_sum = log_sum[-1]
    last_seg = segs[-1]
    state_entering = jnp.where((segs == previous)[:, None], jnp.exp(log_sum), 0.0)
    state_leaving = jnp.where(
        (segs == last_seg)[:, None], jnp.exp(last_sum[None, :] - log_sum), 0.0
    )
    carry_decay = jnp.where(last_seg == previous, jnp.exp(last_sum), 0.0)
    places = jnp.arange(segs.shape[0], dtype=jnp.int32)
    same = (segs[:, None] == segs[None, :]) & (places[:, None] >= places[None, :])
    spread = log_sum.T[:, :, None] - log_sum.T[:, None, :]
    decay_mat = jnp.where(
        same[None], HEAD ** (-0.5) * jnp.exp(jnp.where(same[None], spread, 0.0)), 0.0
    )
    return (state_entering, state_leaving, carry_decay, decay_mat)


def combine(earlier, later):
    return (earlier[0] * later[0], later[0][:, None, None] * earlier[1] + later[1])


def local(tokens, w_query, w_key, w_value, upstream, log_decay, segment):
    rows = tokens.shape[0]
    width = w_query.shape[1]
    heads = width // HEAD
    piece = lax.all_gather(tokens, "head", axis=1, tiled=True)

    def partial_product(weight):
        return jnp.dot(piece, weight, preferred_element_type=jnp.float32)

    query_sum = partial_product(w_query)
    key_sum = partial_product(w_key)
    value_sum = partial_product(w_value)
    query = query_sum.astype(jnp.bfloat16).reshape(rows, heads, HEAD)
    key_rows = key_sum.astype(jnp.bfloat16).reshape(rows, heads, HEAD)
    value_rows = value_sum.astype(jnp.bfloat16).reshape(rows, heads, HEAD)
    output_gradient = upstream.reshape(rows, heads, HEAD)
    my_index = lax.axis_index("seq")
    first = my_index * rows
    segs = lax.dynamic_slice_in_dim(segment, first, rows)
    before = lax.dynamic_slice_in_dim(segment, jnp.maximum(first - 1, 0), 1)[0]
    previous = jnp.where(my_index > 0, before, jnp.int32(-1))
    state_entering, state_leaving, carry_decay, decay_mat = block_factors(log_decay, segs, previous)
    scale = HEAD ** (-0.5)
    weighted_keys = (scale * state_leaving[:, :, None] * key_rows).astype(jnp.bfloat16)
    segment_state = jnp.einsum(
        "bdw,bdq->dwq", weighted_keys, value_rows, preferred_element_type=jnp.float32
    )
    weighted_queries = (scale * state_entering[:, :, None] * query).astype(jnp.bfloat16)
    following_state = jnp.einsum(
        "bdw,bdq->dwq", weighted_queries, output_gradient, preferred_element_type=jnp.float32
    )
    identity = (jnp.ones_like(carry_decay), jnp.zeros_like(segment_state))
    arriving_state = carried_in((carry_decay, segment_state), "seq", combine, identity, False)[1]
    backward_state = carried_in((carry_decay, following_state), "seq", combine, identity, True)[1]
    upper_limit = lax.Precision.HIGHEST
    score_qk = jnp.einsum("thd,shd->hts", query, key_rows, preferred_element_type=jnp.float32)
    attention_query_key = (decay_mat * score_qk).astype(jnp.bfloat16)
    score_up = jnp.einsum(
        "thd,shd->hts", output_gradient, value_rows, preferred_element_type=jnp.float32
    )
    attention_upstream = (decay_mat * score_up).astype(jnp.bfloat16)
    output_gradient_float = output_gradient.astype(jnp.float32)
    query_gradient = jnp.einsum(
        "wcz,zwm->cwm", attention_upstream, key_rows, preferred_element_type=jnp.float32
    ) + state_entering[:, :, None] * jnp.einsum(
        "pzo,zao->pza", output_gradient_float, arriving_state, precision=upper_limit
    )
    key_gradient = jnp.einsum(
        "voi,ovw->ivw", attention_upstream, query, preferred_element_type=jnp.float32
    ) + state_leaving[:, :, None] * jnp.einsum(
        "ixz,xqz->ixq", value_rows.astype(jnp.float32), backward_state, precision=upper_limit
    )
    value_gradient = jnp.einsum(
        "voi,ovw->ivw", attention_query_key, output_gradient, preferred_element_type=jnp.float32
    ) + state_leaving[:, :, None] * jnp.einsum(
        "dqg,qgf->dqf", key_rows.astype(jnp.float32), backward_state, precision=upper_limit
    )
    grads = jnp.concatenate(
        [
            query_gradient.astype(jnp.bfloat16).reshape(rows, width),
            key_gradient.astype(jnp.bfloat16).reshape(rows, width),
            value_gradient.astype(jnp.bfloat16).reshape(rows, width),
        ],
        axis=1,
    )
    contract = (((0,), (0,)), ((), ()))
    columns = lax.all_to_all(piece, "seq", split_axis=1, concat_axis=0, tiled=True)
    every = lax.all_gather(grads, "seq", axis=0, tiled=True)
    sums = lax.dot_general(columns, every, contract, preferred_element_type=jnp.float32)
    grad_query = sums[:, :width].astype(jnp.bfloat16)
    grad_key = sums[:, width : 2 * width].astype(jnp.bfloat16)
    grad_value = sums[:, 2 * width :].astype(jnp.bfloat16)
    return (grad_query, grad_key, grad_value)


def solution(mesh):
    placed = (
        P("seq", "head"),
        P(None, "head"),
        P(None, "head"),
        P(None, "head"),
        P("seq", "head"),
        P("seq", "head"),
        P(),
    )
    return jax.shard_map(
        local,
        mesh=mesh,
        in_specs=placed,
        out_specs=(P("seq", "head"), P("seq", "head"), P("seq", "head")),
        check_vma=False,
    )
```

profile of v0, /device:TPU:0, one launch (start us, length us, event | category | flops | bytes accessed | tf_op | source)
XLA Modules:
  0.0 217.6 jit_solution(17565093690592653566)
XLA Ops:
  7.2 1.8 copy.124
  9.1 1.3 dynamic_slice.41
  14.0 1.1 copy.160
  15.9 23.7 %all-gather.8.cloned.1.call-done = bf16[128,4096]{0,1:T(8,128)(2,1)} async-done(((bf16[128,1024]{0,1:T(8,128)(2,1)}), bf16[128,4096]{0,1:T(8,128)(2,1)}) %all-gather.8.cloned.1.call-update) | async-done | bytes 1048592 | tf_op jit(solution)/shard_map/all_gather | solution.py:55
  39.6 5.1 %convolution_convert_fusion.2 = bf16[128,1024]{1,0:T(8,128)(2,1)S(1)} fusion(bf16[128,4096]{0,1:T(8,128)(2,1)} %all-gather.8.cloned.1.call-done, bf16[4096,1024]{1,0:T(8,128)(2,1)} %param.12), kind=kOutput, calls=%fused_computation.24 | convolution fusion | flops 1073872896 | bytes 9699328 | tf_op jit(solution)/shard_map/dot_general | solution.py:58
  46.0 11.7 %all-gather.2 = bf16[8,1,8]{2,1,0:T(2,128)(2,1)S(1)} all-gather(bf16[1,1,8]{2,1,0:T(2,128)(2,1)S(1)} %get-tuple-element.312), channel_id=1, replica_groups=mesh['seq'=8,'head'=4] {'seq'}, dimensions={0}, use_global_device_ids=true | all-gather | bytes 144 | tf_op jit(solution)/shard_map/all_gather | solution.py:12
  57.9 4.7 %convolution_convert_fusion.5 = bf16[128,1024]{1,0:T(8,128)(2,1)S(1)} fusion(bf16[128,4096]{0,1:T(8,128)(2,1)S(1)} %copy-done, bf16[4096,1024]{1,0:T(8,128)(2,1)} %param.13), kind=kOutput, calls=%fused_computation.27 | convolution fusion | flops 1073872896 | bytes 9699328 | tf_op jit(solution)/shard_map/dot_general | solution.py:58
  62.8 4.7 %fusion.15 = bf16[16,8,8,128]{3,2,1,0:T(8,128)(2,1)S(1)} fusion(bf16[128,4096]{0,1:T(8,128)(2,1)S(1)} %copy-done, bf16[4096,1024]{1,0:T(8,128)(2,1)} %param.14), kind=kOutput, calls=%fused_computation.33 | convolution fusion | flops 1073872896 | bytes 9699328 | tf_op jit(solution)/shard_map/dot_general | solution.py:58
  68.8 6.5 %all-gather.14.cloned.1.call-done = bf16[64,128,128]{2,1,0:T(8,128)(2,1)} async-done(((bf16[8,128,128]{2,1,0:T(8,128)(2,1)}), bf16[64,128,128]{2,1,0:T(8,128)(2,1)}) %all-gather.14.cloned.1.call-update) | async-done | bytes 2097168 | tf_op jit(solution)/shard_map/all_gather | solution.py:12
  75.2 9.1 %while.31 = (s32[]{:T(128)}, f32[8,128,128]{2,1,0:T(8,128)S(1)}, s32[]{:T(128)}, bf16[8,8]{1,0:T(8,128)(2,1)S(1)}, bf16[8,8,128,128]{3,2,1,0:T(8,128)(2,1)}, /*index=5*/s32[]{:T(128)}, s32[]{:T(128)}, s32[]{:T(128)}, s32[]{:T(128)}) while((s32[]{:T(128)}, f32[8,128,128]{2,1,0:T(8,128)S(1)}, s32[]{:T(128)}, ...), condition=%wide.region_4.5_spmd.clone, body=%wide.region_3.4_spmd.clone.sunk | while | flops 655376 | bytes 1310975 | solution.py:26
  76.4 1.1 fusion.60
  77.5 1.1 fusion.60
  78.6 1.1 fusion.60
  79.8 1.1 fusion.60
  80.9 1.1 fusion.60
  82.1 1.1 fusion.60
  83.2 1.1 fusion.60
  84.3 1.5 fusion.8
  85.8 1.4 fusion.9
  87.2 2.3 %fusion.11 = bf16[128,8,128]{0,2,1:T(8,128)(2,1)} fusion(f32[128,8,128]{0,2,1:T(8,128)} %fusion.9, bf16[128,8,128]{0,2,1:T(8,128)(2,1)S(1)} %bitcast.118, bf16[128,8,128]{0,2,1:T(8,128)(2,1)S(1)} %bitcast.121, bf16[128,8,128]{0,2,1:T(8,128)(2,1)S(1)} %bitcast.113, f32[8,128]{1,0:T(8,128)S(1)} %copy.126, pred[128,128]{0,1:T(8,128)(4,1)S(1)} %fusion.29), kind=kOutput, calls=%fused_computation.29 | convolution fusion | flops 68157440 | bytes 1593344 | tf_op jit(solution)/shard_map/voi,ovw->ivw/dot_general | solution.py:103
  89.5 15.9 %all-gather.12.cloned.1.call-done = bf16[64,128,128]{2,1,0:T(8,128)(2,1)} async-done(((bf16[8,128,128]{2,1,0:T(8,128)(2,1)}), bf16[64,128,128]{2,1,0:T(8,128)(2,1)}) %all-gather.12.cloned.1.call-update) | async-done | bytes 2097168 | tf_op jit(solution)/shard_map/all_gather | solution.py:12
  105.4 9.0 %while.30 = (s32[]{:T(128)}, f32[8,128,128]{2,1,0:T(8,128)S(1)}, s32[]{:T(128)}, bf16[8,8]{1,0:T(8,128)(2,1)S(1)}, bf16[8,8,128,128]{3,2,1,0:T(8,128)(2,1)}, /*index=5*/s32[]{:T(128)}, s32[]{:T(128)}) while((s32[]{:T(128)}, f32[8,128,128]{2,1,0:T(8,128)S(1)}, s32[]{:T(128)}, bf16[8,8]{1,0:T(8,128)(2,1)S(1)}, ...), condition=%wide.region_2.3_spmd.clone, body=%wide.region_1.2_spmd.clone.sunk | while | flops 655372 | bytes 1310913 | solution.py:26
  106.5 1.1 fusion.59
  108.8 1.1 fusion.59
  111.1 1.1 fusion.59
  115.4 1.9 pad_maximum_fusion
  117.3 55.8 %all_to_all.19 = bf16[128,8,512]{0,2,1:T(8,128)(2,1)S(1)} all-to-all(bf16[128,8,512]{0,2,1:T(8,128)(2,1)S(1)} %bitcast.110), channel_id=1, replica_groups=mesh['seq'=8,'head'=4] {'seq'}, dimensions={1} | all-to-all | bytes 2097152 | tf_op jit(solution)/shard_map/all_to_all | solution.py:117
  173.6 26.8 %all-gather.10.cloned.1.call-done = bf16[1024,3072]{0,1:T(8,128)(2,1)} async-done(((bf16[128,3072]{0,1:T(8,128)(2,1)}), bf16[1024,3072]{0,1:T(8,128)(2,1)}) %all-gather.10.cloned.1.call-update) | async-done | bytes 6291472 | tf_op jit(solution)/shard_map/all_gather | solution.py:118
  200.4 6.4 %fusion.2 = bf16[512,3072]{0,1:T(8,128)(2,1)S(1)} fusion(bf16[1024,3072]{0,1:T(8,128)(2,1)} %all-gather.10.cloned.1.call-done, bf16[1024,512]{1,0:T(8,128)(2,1)S(1)} %bitcast.123), kind=kOutput, calls=%fused_computation.7 | convolution fusion | flops 3222798336 | bytes 10485760 | tf_op jit(solution)/shard_map/dot_general | solution.py:119
  207.1 1.3 copy.152
  208.4 1.3 copy.151
  209.7 1.3 copy.150
  (57 shorter events, 14.3 us)
Async XLA Ops:
  7.2 32.5 %all-gather.8.cloned.1.call-start = ((), (), s32[]{:S(2)}) async-start(), calls=%async_computation.1 | async-start | bytes 1310720 | tf_op jit(solution)/shard_map/all_gather | solution.py:55
  9.0 66.2 %all-gather.14.cloned.1.call-start = ((), (), s32[]{:S(2)}) async-start(), calls=%async_computation.4 | async-start | bytes 2359296 | tf_op jit(solution)/shard_map/all_gather | solution.py:12
  39.6 18.2 %copy-start = (bf16[128,4096]{0,1:T(8,128)(2,1)S(1)}, bf16[128,4096]{0,1:T(8,128)(2,1)}, u32[]{:S(2)}) copy-start(bf16[128,4096]{0,1:T(8,128)(2,1)} %all-gather.8.cloned.1.call-done) | copy-start | bytes 3145732
  45.9 59.5 %all-gather.12.cloned.1.call-start = ((), (), s32[]{:S(2)}) async-start(), calls=%async_computation.3 | async-start | bytes 2359296 | tf_op jit(solution)/shard_map/all_gather | solution.py:12
  68.5 132.0 %all-gather.10.cloned.1.call-start = ((), (), s32[]{:S(2)}) async-start(), calls=%async_computation.2 | async-start | bytes 7077888 | tf_op jit(solution)/shard_map/all_gather | solution.py:118
  87.2 27.3 %copy-start.1 = (f32[128,8,128]{0,2,1:T(8,128)S(1)}, f32[128,8,128]{0,2,1:T(8,128)}, u32[]{:S(2)}) copy-start(f32[128,8,128]{0,2,1:T(8,128)} %fusion.8) | copy-start | bytes 1572868
Sparse Core Ops, SparseCore 0:
  10.4 29.2 all-gather.7
  46.0 29.1 all-gather.13
  76.8 28.5 all-gather.11
  117.4 82.9 all-gather.9
where the time goes:
time: 219 us; the launch traced here: 218 us
  waiting for transfers between devices  73 us (33%)
  blocking collectives  67.5 us (31%)
  matrix products  29.1 us (13%)
  other arithmetic  21.3 us (10%)
  between operations  15.3 us (7%)
  local copies, waits for them, and re-layouts  10.7 us (5%)
    all_to_all x1, blocking collectives, local(): lax.all_to_all(piece, 'seq', split_axis=1, concat_axis=0, tiled=True)  55.8 us
    all_gather x1, waiting for transfers between devices, local(): every = lax.all_gather(grads, 'seq', axis=0, tiled=True)  26.8 us
    all_gather x1, waiting for transfers between devices, local(): piece = lax.all_gather(tokens, 'head', axis=1, tiled=True)  23.7 us
    all_gather x2, waiting for transfers between devices, carried_in(): lax.all_gather(part.astype(kind), axis)  22.4 us
    select_n x16, other arithmetic, turn(): return jax.tree.map(lambda a, b: jnp.where(reached, a, b), new, before)  17.5 us
    dot_general x3, matrix products, partial_product(): return jnp.dot(piece, weight, preferred_element_type=jnp.float32)  14.5 us
    all_gather x1, blocking collectives, carried_in(): lax.all_gather(part.astype(kind), axis)  11.7 us
    unnamed x10, local copies, waits for them, and re-layouts  6.52 us
  transfers between devices with their start and end apart: 4, of which 4 were waited for; matrix products, arithmetic and copies ran while one was open for 14% of the time, Pallas kernels for 0%

commit v1 on v0

--- a/solution.py
+++ b/solution.py
@@ -114,7 +114,10 @@
         axis=1,
     )
     contract = (((0,), (0,)), ((), ()))
-    columns = lax.all_to_all(piece, "seq", split_axis=1, concat_axis=0, tiled=True)
+    columns = jnp.concatenate(
+        lax.all_to_all(jnp.stack(jnp.split(piece, lax.axis_size("seq"), axis=1)), "seq", 0, 0),
+        axis=0,
+    )
     every = lax.all_gather(grads, "seq", axis=0, tiled=True)
     sums = lax.dot_general(columns, every, contract, preferred_element_type=jnp.float32)
     grad_query = sums[:, :width].astype(jnp.bfloat16)

time: 219 us -> 216 us (0.986)
  local copies, waits for them, and re-layouts: 10.7 us -> 6.04 us
    unnamed x10 -> x13, local copies, waits for them, and re-layouts: 6.52 us -> 0.88 us
where the time goes in v1:
time: 216 us; the launch traced here: 215 us
  waiting for transfers between devices  74.8 us (35%)
  blocking collectives  67.5 us (31%)
  matrix products  29.3 us (14%)
  other arithmetic  21.3 us (10%)
  between operations  15.3 us (7%)
  local copies, waits for them, and re-layouts  6.04 us (3%)
    all_to_all x1, blocking collectives, local(): lax.all_to_all(jnp.stack(jnp.split(piece, lax.axis_size('seq'), axis=1)),...  55.8 us
    all_gather x1, waiting for transfers between devices, local(): every = lax.all_gather(grads, 'seq', axis=0, tiled=True)  27.3 us
    all_gather x1, waiting for transfers between devices, local(): piece = lax.all_gather(tokens, 'head', axis=1, tiled=True)  24.3 us
    all_gather x2, waiting for transfers between devices, carried_in(): lax.all_gather(part.astype(kind), axis)  22.4 us
    select_n x16, other arithmetic, turn(): return jax.tree.map(lambda a, b: jnp.where(reached, a, b), new, before)  17.5 us
    dot_general x3, matrix products, partial_product(): return jnp.dot(piece, weight, preferred_element_type=jnp.float32)  14.4 us
    all_gather x1, blocking collectives, carried_in(): lax.all_gather(part.astype(kind), axis)  11.7 us
    dot_general x1, matrix products, local(): lax.dot_general(columns, every, contract, preferred_element_type=jnp.floa...  6.6 us
  transfers between devices with their start and end apart: 4, of which 4 were waited for; matrix products, arithmetic and copies ran while one was open for 14% of the time, Pallas kernels for 0%

profile of v1, /device:TPU:0, one launch (start us, length us, event | category | flops | bytes accessed | tf_op | source)
XLA Modules:
  0.0 214.9 jit_solution(16309622872515801517)
XLA Ops:
  8.0 1.3 dynamic_slice.41
  12.9 1.1 copy.113
  14.8 24.3 %all-gather.8.cloned.1.call-done = bf16[128,4096]{1,0:T(8,128)(2,1)} async-done(((bf16[128,1024]{1,0:T(8,128)(2,1)}), bf16[128,4096]{1,0:T(8,128)(2,1)}) %all-gather.8.cloned.1.call-update) | async-done | bytes 1048592 | tf_op jit(solution)/shard_map/all_gather | solution.py:55
  39.1 5.0 %convolution_convert_fusion.2 = bf16[128,1024]{1,0:T(8,128)(2,1)S(1)} fusion(bf16[128,4096]{1,0:T(8,128)(2,1)} %all-gather.8.cloned.1.call-done, bf16[4096,1024]{1,0:T(8,128)(2,1)} %param.12), kind=kOutput, calls=%fused_computation.23 | convolution fusion | flops 1073872896 | bytes 9699328 | tf_op jit(solution)/shard_map/dot_general | solution.py:58
  45.4 11.7 %all-gather.2 = bf16[8,1,8]{2,1,0:T(2,128)(2,1)S(1)} all-gather(bf16[1,1,8]{2,1,0:T(2,128)(2,1)S(1)} %get-tuple-element.297), channel_id=1, replica_groups=mesh['seq'=8,'head'=4] {'seq'}, dimensions={0}, use_global_device_ids=true | all-gather | bytes 144 | tf_op jit(solution)/shard_map/all_gather | solution.py:12
  57.3 4.7 %convolution_convert_fusion.5 = bf16[128,1024]{1,0:T(8,128)(2,1)S(1)} fusion(bf16[128,4096]{1,0:T(8,128)(2,1)S(1)} %copy-done, bf16[4096,1024]{1,0:T(8,128)(2,1)} %param.13), kind=kOutput, calls=%fused_computation.26 | convolution fusion | flops 1073872896 | bytes 9699328 | tf_op jit(solution)/shard_map/dot_general | solution.py:58
  62.1 4.7 %fusion.14 = bf16[16,8,8,128]{3,2,1,0:T(8,128)(2,1)S(1)} fusion(bf16[128,4096]{1,0:T(8,128)(2,1)S(1)} %copy-done, bf16[4096,1024]{1,0:T(8,128)(2,1)} %param.14), kind=kOutput, calls=%fused_computation.32 | convolution fusion | flops 1073872896 | bytes 9699328 | tf_op jit(solution)/shard_map/dot_general | solution.py:58
  68.1 6.5 %all-gather.14.cloned.1.call-done = bf16[64,128,128]{2,1,0:T(8,128)(2,1)} async-done(((bf16[8,128,128]{2,1,0:T(8,128)(2,1)}), bf16[64,128,128]{2,1,0:T(8,128)(2,1)}) %all-gather.14.cloned.1.call-update) | async-done | bytes 2097168 | tf_op jit(solution)/shard_map/all_gather | solution.py:12
  74.6 9.1 %while.31 = (s32[]{:T(128)}, f32[8,128,128]{2,1,0:T(8,128)S(1)}, s32[]{:T(128)}, bf16[8,8]{1,0:T(8,128)(2,1)S(1)}, bf16[8,8,128,128]{3,2,1,0:T(8,128)(2,1)}, /*index=5*/s32[]{:T(128)}, s32[]{:T(128)}, s32[]{:T(128)}, s32[]{:T(128)}) while((s32[]{:T(128)}, f32[8,128,128]{2,1,0:T(8,128)S(1)}, s32[]{:T(128)}, ...), condition=%wide.region_4.5_spmd.clone, body=%wide.region_3.4_spmd.clone.sunk | while | flops 655376 | bytes 1310975 | solution.py:26
  75.8 1.1 fusion.67
  76.9 1.1 fusion.67
  78.1 1.1 fusion.67
  79.2 1.1 fusion.67
  80.3 1.1 fusion.67
  81.5 1.1 fusion.67
  82.6 1.1 fusion.67
  83.7 1.5 fusion.7
  85.2 1.4 fusion.8
  86.6 2.3 %fusion.10 = bf16[128,8,128]{0,2,1:T(8,128)(2,1)} fusion(f32[128,8,128]{0,2,1:T(8,128)} %fusion.8, bf16[128,8,128]{0,2,1:T(8,128)(2,1)S(1)} %bitcast.144, bf16[128,8,128]{0,2,1:T(8,128)(2,1)S(1)} %bitcast.147, bf16[128,8,128]{0,2,1:T(8,128)(2,1)S(1)} %bitcast.140, f32[8,128]{1,0:T(8,128)S(1)} %copy.83, pred[128,128]{0,1:T(8,128)(4,1)S(1)} %fusion.36), kind=kOutput, calls=%fused_computation.28 | convolution fusion | flops 68157440 | bytes 1593344 | tf_op jit(solution)/shard_map/voi,ovw->ivw/dot_general | solution.py:103
  88.9 15.9 %all-gather.12.cloned.1.call-done = bf16[64,128,128]{2,1,0:T(8,128)(2,1)} async-done(((bf16[8,128,128]{2,1,0:T(8,128)(2,1)}), bf16[64,128,128]{2,1,0:T(8,128)(2,1)}) %all-gather.12.cloned.1.call-update) | async-done | bytes 2097168 | tf_op jit(solution)/shard_map/all_gather | solution.py:12
  104.8 9.0 %while.30 = (s32[]{:T(128)}, f32[8,128,128]{2,1,0:T(8,128)S(1)}, s32[]{:T(128)}, bf16[8,8]{1,0:T(8,128)(2,1)S(1)}, bf16[8,8,128,128]{3,2,1,0:T(8,128)(2,1)}, /*index=5*/s32[]{:T(128)}, s32[]{:T(128)}) while((s32[]{:T(128)}, f32[8,128,128]{2,1,0:T(8,128)S(1)}, s32[]{:T(128)}, bf16[8,8]{1,0:T(8,128)(2,1)S(1)}, ...), condition=%wide.region_2.3_spmd.clone, body=%wide.region_1.2_spmd.clone.sunk | while | flops 655372 | bytes 1310913 | solution.py:26
  106.0 1.1 fusion.66
  107.1 1.1 fusion.66
  108.2 1.1 fusion.66
  109.4 1.1 fusion.66
  110.5 1.1 fusion.66
  111.6 1.1 fusion.66
  114.8 1.9 pad_maximum_fusion
  116.8 55.8 %all_to_all.5 = bf16[8,128,512]{2,1,0:T(8,128)(2,1)S(1)} all-to-all(bf16[8,128,512]{2,1,0:T(8,128)(2,1)S(1)} %fusion.28), channel_id=1, replica_groups=mesh['seq'=8,'head'=4] {'seq'}, dimensions={0} | all-to-all | bytes 2097152 | tf_op jit(solution)/shard_map/all_to_all | solution.py:118
  172.7 27.3 %all-gather.10.cloned.1.call-done = bf16[1024,3072]{0,1:T(8,128)(2,1)} async-done(((bf16[128,3072]{0,1:T(8,128)(2,1)}), bf16[1024,3072]{0,1:T(8,128)(2,1)}) %all-gather.10.cloned.1.call-update) | async-done | bytes 6291472 | tf_op jit(solution)/shard_map/all_gather | solution.py:121
  200.0 6.6 %convolution_convert_fusion = bf16[512,3072]{1,0:T(8,128)(2,1)S(1)} fusion(bf16[1024,512]{1,0:T(8,128)(2,1)S(1)} %bitcast.149, bf16[1024,3072]{0,1:T(8,128)(2,1)} %all-gather.10.cloned.1.call-done), kind=kOutput, calls=%fused_computation.6 | convolution fusion | flops 3222798336 | bytes 10485760 | tf_op jit(solution)/shard_map/dot_general | solution.py:122
  206.6 1.7 fusion.41
  (60 shorter events, 11.0 us)
Async XLA Ops:
  7.2 31.9 %all-gather.8.cloned.1.call-start = ((), (), s32[]{:S(2)}) async-start(), calls=%async_computation.1 | async-start | bytes 1310720 | tf_op jit(solution)/shard_map/all_gather | solution.py:55
  7.9 66.7 %all-gather.14.cloned.1.call-start = ((), (), s32[]{:S(2)}) async-start(), calls=%async_computation.4 | async-start | bytes 2359296 | tf_op jit(solution)/shard_map/all_gather | solution.py:12
  39.1 18.2 %copy-start = (bf16[128,4096]{1,0:T(8,128)(2,1)S(1)}, bf16[128,4096]{1,0:T(8,128)(2,1)}, u32[]{:S(2)}) copy-start(bf16[128,4096]{1,0:T(8,128)(2,1)} %all-gather.8.cloned.1.call-done) | copy-start | bytes 3145732
  45.3 59.5 %all-gather.12.cloned.1.call-start = ((), (), s32[]{:S(2)}) async-start(), calls=%async_computation.3 | async-start | bytes 2359296 | tf_op jit(solution)/shard_map/all_gather | solution.py:12
  67.8 132.2 %all-gather.10.cloned.1.call-start = ((), (), s32[]{:S(2)}) async-start(), calls=%async_computation.2 | async-start | bytes 7077888 | tf_op jit(solution)/shard_map/all_gather | solution.py:121
  86.6 27.3 %copy-start.1 = (f32[128,8,128]{0,2,1:T(8,128)S(1)}, f32[128,8,128]{0,2,1:T(8,128)}, u32[]{:S(2)}) copy-start(f32[128,8,128]{0,2,1:T(8,128)} %fusion.7) | copy-start | bytes 1572868
Sparse Core Ops, SparseCore 0:
  9.8 29.2 all-gather.7
  45.5 29.1 all-gather.13
  76.2 28.5 all-gather.11
  116.8 83.1 all-gather.9
